TPU v7x, 512 devices: a whole 4x8x8 slice. The times are simulated.
512 devices in a mesh: grid: 64 (over y, z_hi, core), vec: 8 (over x, z_lo).
Axes of the slice: x: 4, y: 8, z: 8 (z_hi: 4, z_lo: 2; z = z_hi * 2 + z_lo), core: 2. Of those that a mesh axis runs over, the one named last changes fastest.
Arguments:
- tgt_coords: float32 [3, 8192], P(None, 'grid'), may hold values from 0 to 1
- src_coords: float32 [3, 8192], P(None, 'grid'), may hold values from 0 to 1
- src_values: float32 [2048, 8192], P('vec', 'grid'), may hold values from -0.26516503 to 0.26516503
- grad_vectors: float32 [3, 2048, 8192], P(None, 'vec', 'grid'), may hold values from -0.75 to 0.75
Outputs:
- interaction: float32 [2048, 2048], P('grid', 'vec')
All inputs are finite; a program needn't handle non-finite values.
Results may differ from a plain program's by a relative error of at most 0.00023.
Values sent between devices are 32-bit elements; how exact they have to be, the bound alone decides.
No kernel may reach another device: no remote copies, remote signals or barrier semaphores. Data moves between devices by JAX's collectives and lax.ppermute only.
A program may use at most 64 MiB of HBM per device.

v0:
```python
import math
import jax
import jax.numpy as jnp
from jax import lax
from jax.sharding import PartitionSpec as P

stiff = 1.0
soft = 0.05


def in_one_piece(arrays, axis, dim, along):
    ends, at = ([], 0)
    for a in arrays[:-1]:
        at += a.shape[along]
        ends.append(at)
    both = jnp.concatenate(arrays, axis=along)
    return tuple(jnp.split(lax.all_gather(both, axis, axis=dim, tiled=True), ends, axis=along))


def cut_along(array, dim, peers):
    shape = array.shape
    blocks = array.reshape(*shape[:dim], peers, shape[dim] // peers, *shape[dim + 1 :])
    return jnp.moveaxis(blocks, dim, 0)


def sum_at_owner(array, axis, dim):
    blocks = cut_along(array, dim, lax.axis_size(axis))
    arrived = lax.all_to_all(blocks, axis, split_axis=0, concat_axis=0, tiled=True)
    return arrived.sum(axis=0)


def pair_kernel(targets, sources):
    diff = targets[:, :, None] - sources[:, None, :]
    dist2 = jnp.sum(diff * diff, axis=0)
    scale = 0.5 / ((1.0 + stiff * jnp.sqrt(dist2)) ** 2 * jnp.sqrt(dist2 + soft * soft))
    return diff * scale[None, :, :]


def body(tgt_coords, src_coords, src_values, grad_vectors):
    width = src_values.shape[0]
    tgt_rows = tgt_coords.shape[1]
    gathered = lax.all_gather(grad_vectors, "vec", axis=1, tiled=True)
    start_sum = jnp.zeros((3, tgt_rows, width), jnp.float32)
    total = start_sum
    coords, values = in_one_piece((src_coords, src_values), "grid", 1, 0)
    count = coords.shape[1]
    block_len = math.gcd(count, 512)
    nblocks = count // block_len
    coord_blocks = coords.reshape(3, nblocks, block_len).transpose(1, 0, 2)
    value_blocks = values.reshape(width, nblocks, block_len).transpose(1, 0, 2)

    def inner(carry, items):
        cblock, vblock = items
        kern = pair_kernel(tgt_coords, cblock)
        carry = carry + jnp.einsum("cts,qs->ctq", kern, vblock, precision=lax.Precision.HIGHEST)
        return (carry, None)

    total, _ = lax.scan(inner, total, (coord_blocks, value_blocks))
    partial_value = jnp.einsum("cpt,ctq->pq", gathered, total, precision=lax.Precision.HIGHEST)
    return sum_at_owner(partial_value, "grid", 0)


def solution(mesh):
    return jax.shard_map(
        body,
        mesh=mesh,
        in_specs=(P(None, "grid"), P(None, "grid"), P("vec", "grid"), P(None, "vec", "grid")),
        out_specs=P("grid", "vec"),
        check_vma=False,
    )
```

profile of v0, /device:TPU:24, one launch (start us, length us, event | category | flops | bytes accessed | tf_op | source)
XLA Modules:
  0.0 294.5 jit_solution(4307227119990213914)
XLA Ops:
  6.5 1.0 copy.7
  7.5 0.8 copy.6
  8.3 0.8 pad_maximum_fusion
  9.2 0.7 all-gather.5.cloned.1.call-update
  9.9 126.4 %all-gather.3.cloned.1.call-done = f32[259,8192]{0,1:T(8,128)} async-done(((f32[259,128]{0,1:T(8,128)}), f32[259,8192]{0,1:T(8,128)}) %all-gather.3.cloned.1.call-update) | async-done | bytes 8486928 | tf_op jit(solution)/shard_map/all_gather | solution.py:17
  136.3 4.4 %split.8 = f32[3,8192]{0,1:T(8,128)} slice(f32[259,8192]{0,1:T(8,128)} %all-gather.3.cloned.1.call-done), slice={[0:3], [0:8192]} | slice | bytes 196608 | tf_op jit(solution)/shard_map/split | solution.py:17
  140.7 2.8 copy.8
  143.6 10.0 %split.9 = f32[256,8192]{0,1:T(8,128)} slice(f32[259,8192]{0,1:T(8,128)} %all-gather.3.cloned.1.call-done), slice={[3:259], [0:8192]} | slice | bytes 16777216 | tf_op jit(solution)/shard_map/split | solution.py:17
  153.6 38.8 %while.11 = (s32[]{:T(128)}, f32[3,128,256]{2,1,0:T(8,128)S(1)}, f32[3,128]{1,0:T(4,128)S(1)}, f32[16,3,512]{2,1,0:T(4,128)S(1)}, f32[16,256,512]{1,2,0:T(8,128)}, /*index=5*/s32[]{:T(128)}, s32[]{:T(128)}) while((s32[]{:T(128)}, f32[3,128,256]{2,1,0:T(8,128)S(1)}, f32[3,128]{1,0:T(4,128)S(1)}, f32[16,3,512]{2,1,0:T(4,128)S(1)}, ...), condition=%wide.region_2.3_spmd.clone, body=%wide.region_0.2_spmd.clone.sunk | while | flops 605421568 | bytes 2387047 | solution.py:58
  153.7 0.2 multiply_divide_fusion.2
  153.9 2.0 convolution_add_fusion.2
  156.2 0.2 multiply_divide_fusion.2
  156.3 2.1 convolution_add_fusion.2
  158.8 2.1 convolution_add_fusion.2
  161.2 2.0 convolution_add_fusion.2
  163.6 2.0 convolution_add_fusion.2
  166.1 2.0 convolution_add_fusion.2
  168.5 2.0 convolution_add_fusion.2
  170.9 2.0 convolution_add_fusion.2
  173.3 2.1 convolution_add_fusion.2
  175.8 2.1 convolution_add_fusion.2
  178.2 2.0 convolution_add_fusion.2
  180.6 2.0 convolution_add_fusion.2
  183.1 2.0 convolution_add_fusion.2
  185.5 2.0 convolution_add_fusion.2
  187.9 2.1 convolution_add_fusion.2
  190.4 2.1 convolution_add_fusion.2
  192.4 18.9 %all-gather.5.cloned.1.call-done = f32[3,2048,128]{2,1,0:T(8,128)} async-done(((f32[3,256,128]{2,1,0:T(8,128)}), f32[3,2048,128]{2,1,0:T(8,128)}) %all-gather.5.cloned.1.call-update) | async-done | bytes 3145744 | tf_op jit(solution)/shard_map/all_gather | solution.py:42
  211.3 7.1 %convolution_bitcast_fusion = f32[2048,256]{0,1:T(8,128)S(1)} fusion(f32[3,128,256]{2,1,0:T(8,128)S(1)} %get-tuple-element.32, f32[3,2048,128]{2,1,0:T(8,128)} %all-gather.5.cloned.1.call-done), kind=kOutput, calls=%fused_computation.12 | convolution fusion | flops 2415919104 | bytes 5636096 | tf_op jit(solution)/shard_map/cpt,ctq->pq/dot_general | solution.py:59
  218.5 1.9 copy.11
  220.3 66.6 %all_to_all.5 = f32[64,32,256]{2,1,0:T(8,128)S(1)} all-to-all(f32[64,32,256]{2,1,0:T(8,128)} %bitcast.25), channel_id=1, replica_groups=mesh['grid'=64,'vec'=8] {'grid'}, dimensions={0} | all-to-all | bytes 4194304 | tf_op jit(solution)/shard_map/all_to_all | solution.py:28
  286.9 0.8 reduce_sum.18
  (52 shorter events, 5.0 us)
Async XLA Ops:
  6.5 129.8 %all-gather.3.cloned.1.call-start = ((), (), s32[]{:S(2)}) async-start(), calls=%async_computation.1 | async-start | bytes 12779520 | tf_op jit(solution)/shard_map/all_gather | solution.py:17
  9.2 202.2 %all-gather.5.cloned.1.call-start = ((), (), s32[]{:S(2)}) async-start(), calls=%async_computation.2 | async-start | bytes 3538944 | tf_op jit(solution)/shard_map/all_gather | solution.py:42
  143.6 10.0 %copy-start = (f32[3,128]{1,0:T(4,128)S(1)}, f32[3,128]{1,0:T(4,128)}, u32[]{:S(2)}) copy-start(f32[3,128]{1,0:T(4,128)} %param.6) | copy-start | bytes 4612
Sparse Core Ops, SparseCore 0:
  10.6 125.6 all-gather.2
  138.4 72.8 all-gather.4
where the time goes:
time: 296 us; the launch traced here: 294 us
  waiting for transfers between devices  146 us (49%)
  blocking collectives  66.6 us (22%)
  matrix products  39.9 us (13%)
  local copies, waits for them, and re-layouts  21 us (7%)
  between operations  13.4 us (5%)
  other arithmetic  6.7 us (2%)
    all_gather x1, waiting for transfers between devices, in_one_piece(): lax.all_gather(both, axis, axis=dim, tiled=True)  126 us
    all_to_all x1, blocking collectives, sum_at_owner(): lax.all_to_all(blocks, axis, split_axis=0, concat_axis=0, tiled=True)  66.6 us
    dot_general x16, matrix products, inner(): jnp.einsum('cts,qs->ctq', kern, vblock, precision=lax.Precision.HIGHEST)  32.8 us
    all_gather x1, waiting for transfers between devices, body(): gathered = lax.all_gather(grad_vectors, 'vec', axis=1, tiled=True)  18.9 us
    split x2, local copies, waits for them, and re-layouts, in_one_piece(): jnp.split(lax.all_gather(both, axis, axis=dim, tiled=True), ends, axis=al...  14.4 us
    dot_general x1, matrix products, body(): jnp.einsum('cpt,ctq->pq', gathered, total, precision=lax.Precision.HIGHEST)  7.14 us
  transfers between devices with their start and end apart: 2, of which 2 were waited for; matrix products, arithmetic and copies ran while one was open for 19% of the time, Pallas kernels for 0%

commit v1 on v0

--- a/solution.py
+++ b/solution.py
@@ -6,6 +6,13 @@
 
 stiff = 1.0
 soft = 0.05
+
+
+def gather_over(x, name, dim):
+    size = lax.axis_size(name)
+    shards = jnp.stack([x for _ in range(size)])
+    shards = lax.all_to_all(shards, name, split_axis=0, concat_axis=0)
+    return jnp.concatenate(shards, axis=dim)
 
 
 def in_one_piece(arrays, axis, dim, along):
@@ -39,7 +46,7 @@
 def body(tgt_coords, src_coords, src_values, grad_vectors):
     width = src_values.shape[0]
     tgt_rows = tgt_coords.shape[1]
-    gathered = lax.all_gather(grad_vectors, "vec", axis=1, tiled=True)
+    gathered = gather_over(grad_vectors, "vec", 1)
     start_sum = jnp.zeros((3, tgt_rows, width), jnp.float32)
     total = start_sum
     coords, values = in_one_piece((src_coords, src_values), "grid", 1, 0)

time: 296 us -> 273 us (0.922)
  waiting for transfers between devices: 146 us -> 114 us
  local copies, waits for them, and re-layouts: 21 us -> 28 us
  starting transfers between devices: 0.04 us -> 6.11 us
  blocking collectives: 66.6 us -> 62.3 us
    all_gather x1, waiting for transfers between devices: 126 us -> 69.6 us  [in_one_piece(): lax.all_gather(both, axis, axis=dim, tiled=True)]
    all_to_all x0 -> x1, waiting for transfers between devices: none -> 44.6 us  [gather_over(): shards = lax.all_to_all(shards, name, split_axis=0, concat_axis=0)]
    all_gather x1 -> x0, waiting for transfers between devices: 18.9 us -> none  [body(): gathered = lax.all_gather(grad_vectors, 'vec', axis=1, tiled=True)]
    all_to_all x0 -> x1, starting transfers between devices: none -> 6.11 us  [gather_over(): shards = lax.all_to_all(shards, name, split_axis=0, concat_axis=0)]
    all_to_all x1, blocking collectives: 66.6 us -> 62.3 us  [sum_at_owner(): lax.all_to_all(blocks, axis, split_axis=0, concat_axis=0, tiled=True)]
    reshape x0 -> x1, local copies, waits for them, and re-layouts: none -> 3.87 us  [gather_over(): return jnp.concatenate(shards, axis=dim)]
    another operation x0 -> x1, local copies, waits for them, and re-layouts: none -> 2.99 us  [gather_over(): shards = jnp.stack([x for _ in range(size)])]
  transfers between devices with their start and end apart: 2 -> 2, of which waited for: 2 -> 2; matrix products, arithmetic and copies ran while one was open for 19% -> 3% of each run, Pallas kernels for 0% -> 0%
where the time goes in v1:
time: 273 us; the launch traced here: 271 us
  waiting for transfers between devices  114 us (42%)
  blocking collectives  62.3 us (23%)
  matrix products  39.9 us (15%)
  local copies, waits for them, and re-layouts  28 us (10%)
  between operations  13.4 us (5%)
  other arithmetic  6.7 us (2%)
  starting transfers between devices  6.11 us (2%)
    all_gather x1, waiting for transfers between devices, in_one_piece(): lax.all_gather(both, axis, axis=dim, tiled=True)  69.6 us
    all_to_all x1, blocking collectives, sum_at_owner(): lax.all_to_all(blocks, axis, split_axis=0, concat_axis=0, tiled=True)  62.3 us
    all_to_all x1, waiting for transfers between devices, gather_over(): shards = lax.all_to_all(shards, name, split_axis=0, concat_axis=0)  44.6 us
    dot_general x16, matrix products, inner(): jnp.einsum('cts,qs->ctq', kern, vblock, precision=lax.Precision.HIGHEST)  32.8 us
    split x2, local copies, waits for them, and re-layouts, in_one_piece(): jnp.split(lax.all_gather(both, axis, axis=dim, tiled=True), ends, axis=al...  14.5 us
    dot_general x1, matrix products, body(): jnp.einsum('cpt,ctq->pq', gathered, total, precision=lax.Precision.HIGHEST)  7.14 us
    all_to_all x1, starting transfers between devices, gather_over(): shards = lax.all_to_all(shards, name, split_axis=0, concat_axis=0)  6.11 us
  transfers between devices with their start and end apart: 2, of which 2 were waited for; matrix products, arithmetic and copies ran while one was open for 3% of the time, Pallas kernels for 0%

profile of v1, /device:TPU:24, one launch (start us, length us, event | category | flops | bytes accessed | tf_op | source)
XLA Modules:
  0.0 271.5 jit_solution(3213325539596021698)
XLA Ops:
  6.5 1.0 copy.13
  7.5 0.8 copy.12
  8.3 0.8 pad_maximum_fusion
  9.2 3.0 %stack.2 = f32[8,3,256,128]{3,2,1,0:T(8,128)} broadcast(f32[3,256,128]{2,1,0:T(8,128)} %param.9), dimensions={1,2,3} | broadcast | bytes 3538944 | tf_op jit(solution)/shard_map/stack | solution.py:13
  12.2 6.1 %all-to-all-start = ((f32[8,3,256,128]{3,2,1,0:T(8,128)}), f32[8,3,256,128]{3,2,1,0:T(8,128)}, u32[]{:S(2)}, u32[]{:S(2)}) async-start(f32[8,3,256,128]{3,2,1,0:T(8,128)} %stack.2), calls=%async_computation | async-start | bytes 6291456 | tf_op jit(solution)/shard_map/all_to_all | solution.py:14
  18.3 44.6 %all-to-all-done = f32[8,3,256,128]{3,2,1,0:T(8,128)} async-done(((f32[8,3,256,128]{3,2,1,0:T(8,128)}), f32[8,3,256,128]{3,2,1,0:T(8,128)}, u32[]{:S(2)}, u32[]{:S(2)}) %all-to-all-start) | async-done | bytes 3145760 | tf_op jit(solution)/shard_map/all_to_all | solution.py:14
  62.9 3.9 %copy.16 = f32[3,8,256,128]{3,2,1,0:T(8,128)} copy(f32[3,8,256,128]{3,2,0,1:T(8,128)} %bitcast.4) | data formatting | bytes 6291456 | tf_op jit(solution)/shard_map/reshape | solution.py:15
  66.8 69.6 %all-gather.2.cloned.1.call-done = f32[259,8192]{0,1:T(8,128)} async-done(((f32[259,128]{0,1:T(8,128)}), f32[259,8192]{0,1:T(8,128)}) %all-gather.2.cloned.1.call-update) | async-done | bytes 8486928 | tf_op jit(solution)/shard_map/all_gather | solution.py:24
  136.4 4.5 %split.8 = f32[3,8192]{0,1:T(8,128)} slice(f32[259,8192]{0,1:T(8,128)} %all-gather.2.cloned.1.call-done), slice={[0:3], [0:8192]} | slice | bytes 196608 | tf_op jit(solution)/shard_map/split | solution.py:24
  140.9 2.8 %copy.14 = f32[3,16,512]{2,0,1:T(4,128)S(1)} copy(f32[3,16,512]{0,2,1:T(8,128)} %bitcast.25) | data formatting | bytes 196608 | tf_op jit(solution)/shard_map/reshape | solution.py:56
  143.7 10.0 %split.9 = f32[256,8192]{0,1:T(8,128)} slice(f32[259,8192]{0,1:T(8,128)} %all-gather.2.cloned.1.call-done), slice={[3:259], [0:8192]} | slice | bytes 16777216 | tf_op jit(solution)/shard_map/split | solution.py:24
  153.8 38.8 %while.11 = (s32[]{:T(128)}, f32[3,128,256]{2,1,0:T(8,128)S(1)}, f32[3,128]{1,0:T(4,128)S(1)}, f32[16,3,512]{2,1,0:T(4,128)S(1)}, f32[16,256,512]{1,2,0:T(8,128)}, /*index=5*/s32[]{:T(128)}, s32[]{:T(128)}) while((s32[]{:T(128)}, f32[3,128,256]{2,1,0:T(8,128)S(1)}, f32[3,128]{1,0:T(4,128)S(1)}, f32[16,3,512]{2,1,0:T(4,128)S(1)}, ...), condition=%wide.region_2.3_spmd.clone, body=%wide.region_0.2_spmd.clone.sunk | while | flops 605421568 | bytes 2387047 | solution.py:65
  154.1 2.0 convolution_add_fusion.2
  156.5 2.0 convolution_add_fusion.2
  159.0 2.0 convolution_add_fusion.2
  161.4 2.0 convolution_add_fusion.2
  163.8 2.0 convolution_add_fusion.2
  166.2 2.0 convolution_add_fusion.2
  168.7 2.0 convolution_add_fusion.2
  171.1 2.0 convolution_add_fusion.2
  173.5 2.0 convolution_add_fusion.2
  176.0 2.0 convolution_add_fusion.2
  178.4 2.0 convolution_add_fusion.2
  180.8 2.0 convolution_add_fusion.2
  183.2 2.0 convolution_add_fusion.2
  185.7 2.0 convolution_add_fusion.2
  188.1 2.0 convolution_add_fusion.2
  190.5 2.0 convolution_add_fusion.2
  192.6 7.1 %convolution_bitcast_fusion = f32[2048,256]{0,1:T(8,128)S(1)} fusion(f32[3,128,256]{2,1,0:T(8,128)S(1)} %get-tuple-element.32, f32[3,2048,128]{2,1,0:T(8,128)} %bitcast.27), kind=kOutput, calls=%fused_computation.12 | convolution fusion | flops 2415919104 | bytes 5636096 | tf_op jit(solution)/shard_map/cpt,ctq->pq/dot_general | solution.py:66
  199.7 1.9 copy.18
  201.6 62.3 %all_to_all.10 = f32[64,32,256]{2,1,0:T(8,128)S(1)} all-to-all(f32[64,32,256]{2,1,0:T(8,128)} %bitcast.28), channel_id=1, replica_groups=mesh['grid'=64,'vec'=8] {'grid'}, dimensions={0} | all-to-all | bytes 4194304 | tf_op jit(solution)/shard_map/all_to_all | solution.py:35
  263.9 0.8 reduce_sum.18
  (53 shorter events, 5.3 us)
Async XLA Ops:
  6.5 129.8 %all-gather.2.cloned.1.call-start = ((), (), s32[]{:S(2)}) async-start(), calls=%async_computation.2 | async-start | bytes 12779520 | tf_op jit(solution)/shard_map/all_gather | solution.py:24
  12.2 50.7 %all-to-all-start = ((f32[8,3,256,128]{3,2,1,0:T(8,128)}), f32[8,3,256,128]{3,2,1,0:T(8,128)}, u32[]{:S(2)}, u32[]{:S(2)}) async-start(f32[8,3,256,128]{3,2,1,0:T(8,128)} %stack.2), calls=%async_computation | async-start | bytes 6291456 | tf_op jit(solution)/shard_map/all_to_all | solution.py:14
  143.7 10.0 %copy-start = (f32[3,128]{1,0:T(4,128)S(1)}, f32[3,128]{1,0:T(4,128)}, u32[]{:S(2)}) copy-start(f32[3,128]{1,0:T(4,128)} %param.6) | copy-start | bytes 4612
Sparse Core Ops, SparseCore 0:
  10.6 125.6 all-gather.1
